TPU v7x, 32 devices: a whole 2x2x4 slice. The times are simulated.
32 devices in a mesh: grow: 8 (over y, x, core), gcol: 4 (over z).
Axes of the slice: x: 2, y: 2, z: 4, core: 2. Of those that a mesh axis runs over, the one named last changes fastest.
Arguments:
- eps_static: float32 [12288, 12288], P('grow', 'gcol'), may hold values from -1.8 to 1.8
- eps_imag: float32 [12288, 12288], P('grow', 'gcol'), may hold values from -1.8 to 1.8
- frequency_grid: float32 [3], replicated, may hold values from 0.1 to 2
- band_energy: float32 [32], replicated, may hold values from -2 to 2
- pair_elements: bfloat16 [32, 64, 12288], P('grow', None, 'gcol'), may hold values from -0.0546875 to 0.0546875
Outputs:
- sigma: float32 [3, 64], P(None, 'gcol')
All inputs are finite; a program needn't handle non-finite values.
Results may differ from a plain program's by a relative error of at most 0.0019.
Values may be sent and summed in bfloat16 or wider, within the bound.
A program may use at most 128 MiB of HBM per device.

v0:
```python
import functools

import jax
import jax.numpy as jnp
from jax import lax
from jax.experimental import pallas as pl
from jax.experimental.pallas import tpu as pltpu
from jax.sharding import PartitionSpec as P

LANES = 128
SUB_ROWS = 32
SUB_COLS = 512
DOT_COLS = 256


def bit_flip(index, mask, extent):
    total, bit = 0, 1
    while bit < extent:
        total = total + ((index // bit + mask // bit) % 2) * bit
        bit *= 2
    return total


def body(R, Z, bpd, states, height, breadth, ne,
         freq, energy, es_hbm, ei_hbm, pair_hbm, out,
         kern, colp, rowp, es_buf, ei_buf, sig, part, recv1, recv2, hold,
         eps_sem, own_sem, col_send, col_recv, row_recv, up_send, dn_send,
         s1_send, s1_recv, s2_send, s2_recv, hold_send, hold_recv, give_send):
    r = lax.axis_index("grow")
    z = lax.axis_index("gcol")
    ratio = R // Z
    home = r // ratio
    offset = pl.multiple_of(r % ratio * height, height)
    spc = states // Z
    units = R * bpd
    blocks = 4 * bpd
    rows = height // blocks

    def dev(row, col):
        return dict(device_id={"grow": row, "gcol": col}, device_id_type=pl.DeviceIdType.MESH)

    def eps_copies(block, slot):
        at = pl.multiple_of(block * rows, rows)
        return (pltpu.make_async_copy(es_hbm.at[pl.ds(at, rows), :], es_buf.at[slot], eps_sem.at[0, slot]),
                pltpu.make_async_copy(ei_hbm.at[pl.ds(at, rows), :], ei_buf.at[slot], eps_sem.at[1, slot]))

    own = pltpu.make_async_copy(pair_hbm, colp.at[0], own_sem)
    own.start()
    for copy in eps_copies(0, 0):
        copy.start()

    barrier = pltpu.get_barrier_semaphore()
    for d in range(1, R):
        pl.semaphore_signal(barrier, inc=1, **dev((r + d) % R, z))
    for d in range(1, Z):
        pl.semaphore_signal(barrier, inc=1, **dev(r, (z + d) % Z))
    sig[...] = jnp.zeros_like(sig)
    own.wait()
    pl.semaphore_wait(barrier, R + Z - 2)

    def unit_rows(b):
        return pl.ds(pl.multiple_of(b * states, states), states)

    def col_copy(src_shard, dst_shard, b, row):
        return pltpu.make_async_remote_copy(
            src_ref=colp.at[src_shard, unit_rows(b), :], dst_ref=colp.at[dst_shard, unit_rows(b), :],
            send_sem=col_send.at[dst_shard * bpd + b], recv_sem=col_recv.at[dst_shard * bpd + b],
            **dev(row, z))

    partner = bit_flip(r, 1, R)

    def send_own(b, carry):
        col_copy(0, 1, b, partner).start()
        return carry
    lax.fori_loop(0, bpd, send_own, 0)
    for shard in range(2, R, 2):
        peer = bit_flip(r, shard, R)

        def send_far(b, carry, shard=shard, peer=peer):
            col_copy(0, shard, b, peer).start()
            return carry
        lax.fori_loop(0, bpd, send_far, 0)

    def row_copy(shard, b, u, sems, col):
        ref = rowp.at[shard, unit_rows(b), :]
        return pltpu.make_async_remote_copy(
            src_ref=ref, dst_ref=ref, send_sem=sems.at[u], recv_sem=row_recv.at[u], **dev(r, col))

    side = bpd // 2
    keep = bpd - side
    items = (Z - 1) * side
    stride = 2 if 3 + 2 * (items - 1) < units else 1
    relay_down = home == 0
    relays = jnp.logical_or(relay_down, home == Z - 1)
    ahead = jnp.where(relay_down, z - 1, z + 1)
    has_ahead = jnp.logical_and(relays, jnp.logical_and(ahead >= 0, ahead < Z))
    ahead_col = (ahead + Z) % Z

    def side_copy(d, b):
        dst = hold.at[d, unit_rows(b), :]
        src = hold.at[d - 1, unit_rows(b), :] if not (isinstance(d, int) and d == 0) else colp.at[0, unit_rows(keep + b), :]
        return pltpu.make_async_remote_copy(
            src_ref=src, dst_ref=dst, send_sem=hold_send.at[d * side + b],
            recv_sem=hold_recv.at[d * side + b], **dev(r, ahead_col))

    def give_copy(d, b, k, panel):
        to = panel * ratio + k
        shard = bit_flip(r, to, R)
        return pltpu.make_async_remote_copy(
            src_ref=hold.at[d - 1, unit_rows(b), pl.ds(k * height, height)],
            dst_ref=rowp.at[shard, unit_rows(keep + b), :],
            send_sem=give_send.at[((d - 1) * side + b) * ratio + k],
            recv_sem=row_recv.at[shard * bpd + keep + b], **dev(to, z))

    def relay_item(t, act):
        d, b = t // side + 1, t % side
        panel = jnp.where(relay_down, z + d, z - d)

        @pl.when(jnp.logical_and(relays, jnp.logical_and(panel >= 0, panel < Z)))
        def _():
            act(d, b, (panel + Z) % Z)

    def pass_on(d, b, panel):
        pltpu.make_async_remote_copy(
            src_ref=hold.at[d - 1, unit_rows(b), :], dst_ref=hold.at[d - 1, unit_rows(b), :],
            send_sem=hold_send.at[(d - 1) * side + b], recv_sem=hold_recv.at[(d - 1) * side + b],
            **dev(r, ahead_col)).wait_recv()

        @pl.when(has_ahead)
        def _():
            side_copy(d, b).start()
        for k in range(ratio):
            give_copy(d, b, k, panel).start()

    def settle(d, b, panel):
        @pl.when(has_ahead)
        def _():
            side_copy(d, b).wait_send()
        for k in range(ratio):
            give_copy(d, b, k, panel).wait_send()

    @pl.when(has_ahead)
    def _():
        for b in range(side):
            side_copy(0, b).start()

    def aside(shard, b, group):
        return jnp.logical_and(b >= keep, bit_flip(r, shard, R) // ratio == group)

    goes_up = jnp.logical_and(z >= home, z < Z - 1)
    goes_down = jnp.logical_and(z <= home, z > 0)
    upper = (z + 1) % Z
    lower = (z + Z - 1) % Z

    def comm(u):
        shard, b = u // bpd, u % bpd

        @pl.when(shard >= 1)
        def _():
            col_copy(0, shard, b, partner).wait_recv()

        @pl.when(jnp.logical_and(shard >= 2, shard % 2 == 0))
        def _():
            col_copy(shard, shard + 1, b, partner).start()

        @pl.when(z == home)
        def _():
            local = pltpu.make_async_copy(
                colp.at[shard, unit_rows(b), pl.ds(offset, height)],
                rowp.at[shard, unit_rows(b), :], row_recv.at[u])
            local.start()
            local.wait()

        @pl.when(z != home)
        def _():
            row_copy(shard, b, u, up_send, upper).wait_recv()

        @pl.when(jnp.logical_and(goes_up, jnp.logical_not(aside(shard, b, Z - 1))))
        def _():
            row_copy(shard, b, u, up_send, upper).start()

        @pl.when(jnp.logical_and(goes_down, jnp.logical_not(aside(shard, b, 0))))
        def _():
            row_copy(shard, b, u, dn_send, lower).start()

        @pl.when(jnp.logical_and(jnp.logical_and(u >= 3, (u - 3) % stride == 0),
                                 (u - 3) // stride < items))
        def _():
            relay_item((u - 3) // stride, pass_on)

    diagonal = r * height - z * breadth
    sub_rows = min(SUB_ROWS, rows)
    sub_cols = min(SUB_COLS, breadth)
    col_steps = breadth // sub_cols
    f0, f1, f2 = freq[0], freq[1], freq[2]

    def make_block(block):
        slot = block % 2

        @pl.when(block + 1 < blocks)
        def _():
            for copy in eps_copies(block + 1, 1 - slot):
                copy.start()
        for copy in eps_copies(block, slot):
            copy.wait()
        base = pl.multiple_of(block * rows, rows)

        def chunk(n, carry):
            at_row = pl.multiple_of(n // col_steps * sub_rows, sub_rows)
            at_col = pl.multiple_of(n % col_steps * sub_cols, sub_cols)
            where = (pl.ds(at_row, sub_rows), pl.ds(at_col, sub_cols))
            gap = (lax.broadcasted_iota(jnp.int32, (sub_rows, sub_cols), 0)
                   - lax.broadcasted_iota(jnp.int32, (sub_rows, sub_cols), 1))
            one = jnp.where(gap == at_col - at_row - base - diagonal, 1.0, 0.0)
            static = es_buf[(slot,) + where] - one
            imag = ei_buf[(slot,) + where] - one
            spread = static - imag
            over = imag * imag + 0.25
            under = spread * spread + 0.25
            pole = over * lax.rsqrt(over * under)
            p0, p1, p2 = pole + f0, pole + f1, pole + f2
            p01 = p0 * p1
            scale = -static * pole / (p01 * p2)
            to = (pl.ds(pl.multiple_of(base + at_row, sub_rows), sub_rows), where[1])
            kern[(0,) + to] = (p1 * p2 * scale).astype(jnp.bfloat16)
            kern[(1,) + to] = (p0 * p2 * scale).astype(jnp.bfloat16)
            kern[(2,) + to] = (p01 * scale).astype(jnp.bfloat16)
            return carry
        lax.fori_loop(0, rows // sub_rows * col_steps, chunk, 0)

    width = breadth // bpd
    dot_cols = min(DOT_COLS, width)
    while width % dot_cols:
        dot_cols //= 2

    def piece(number):
        shard, q = number // bpd, number % bpd
        first = bit_flip(r, shard, R) * bpd

        def step(n, carry):
            cols = pl.ds(pl.multiple_of(q * width + n * dot_cols, dot_cols), dot_cols)
            right = colp[shard, :, cols].astype(jnp.float32)
            left = rowp[shard]
            sums = []
            for e in range(ne):
                prod = jnp.dot(left, kern[e, :, cols], preferred_element_type=jnp.float32) * right
                thin = prod[:, :LANES]
                for k in range(1, dot_cols // LANES):
                    thin = thin + prod[:, k * LANES:(k + 1) * LANES]
                total = carry[e]
                for b in range(bpd):
                    miss = jnp.full((8, LANES), freq[e] - energy[first + b], jnp.float32)
                    weight = (1.0 / (1.0 + miss * miss))[:1]
                    total = total + weight * thin[b * states:(b + 1) * states]
                sums.append(total)
            return tuple(sums)
        start = tuple(sig[e] for e in range(ne))
        done = lax.fori_loop(0, width // dot_cols, step, start)
        for e in range(ne):
            sig[e] = done[e]

    def phase_a(u, carry):
        comm(u)
        make_block(2 * u)
        make_block(2 * u + 1)
        return carry
    lax.fori_loop(0, 2 * bpd, phase_a, 0)

    def phase_b(u, carry):
        comm(u)
        piece(2 * (u - 2 * bpd))
        piece(2 * (u - 2 * bpd) + 1)
        return carry
    lax.fori_loop(2 * bpd, 3 * bpd, phase_b, 0)

    def phase_c(u, carry):
        comm(u)
        piece(u - bpd)
        return carry
    lax.fori_loop(3 * bpd, units, phase_c, 0)

    def phase_d(u, carry):
        piece(u - bpd)
        return carry
    lax.fori_loop(units, units + bpd, phase_d, 0)

    for owner in range(Z):
        for e in range(ne):
            part[owner, e] = sig[e, owner * spc:(owner + 1) * spc]

    def s1_copy(d):
        return pltpu.make_async_remote_copy(
            src_ref=part.at[(z + d) % Z], dst_ref=recv1.at[d - 1],
            send_sem=s1_send.at[d - 1], recv_sem=s1_recv.at[d - 1], **dev(r, (z + d) % Z))

    def s2_copy(d, owner):
        return pltpu.make_async_remote_copy(
            src_ref=recv2.at[owner], dst_ref=recv2.at[owner],
            send_sem=s2_send.at[d - 1], recv_sem=s2_recv.at[owner], **dev((r + d) % R, z))

    for d in range(1, Z):
        s1_copy(d).start()

    def drain(u, carry):
        shard, b = u // bpd, u % bpd

        @pl.when(shard >= 1)
        def _():
            col_copy(0, shard, b, partner).wait_send()

        @pl.when(jnp.logical_and(goes_up, jnp.logical_not(aside(shard, b, Z - 1))))
        def _():
            row_copy(shard, b, u, up_send, upper).wait_send()

        @pl.when(jnp.logical_and(goes_down, jnp.logical_not(aside(shard, b, 0))))
        def _():
            row_copy(shard, b, u, dn_send, lower).wait_send()
        return carry
    lax.fori_loop(0, units, drain, 0)

    @pl.when(has_ahead)
    def _():
        for b in range(side):
            side_copy(0, b).wait_send()

    def drain_side(t, carry):
        relay_item(t, settle)
        return carry
    lax.fori_loop(0, items, drain_side, 0)

    mine = part[z]
    for d in range(1, Z):
        s1_copy(d).wait_recv()
        mine = mine + recv1[d - 1]
    recv2[r] = mine
    for d in range(1, R):
        s2_copy(d, r).start()
    for d in range(1, R):
        s2_copy(d, (r + R - d) % R).wait_recv()
    full = recv2[0]
    for owner in range(1, R):
        full = full + recv2[owner]
    out[...] = jnp.sum(full, axis=-1)
    for d in range(1, Z):
        s1_copy(d).wait_send()
    for d in range(1, R):
        s2_copy(d, r).wait_send()


def solution(mesh):
    R, Z = mesh.shape["grow"], mesh.shape["gcol"]

    def shards(eps_static, eps_imag, frequency_grid, band_energy, pair_elements):
        height, breadth = eps_static.shape
        bpd, states, _ = pair_elements.shape
        ne = frequency_grid.shape[0]
        spc = states // Z
        rows = height // (4 * bpd)
        dma = pltpu.SemaphoreType.DMA
        units = R * bpd
        any_space = pl.BlockSpec(memory_space=pl.ANY)
        smem = pl.BlockSpec(memory_space=pltpu.SMEM)
        return pl.pallas_call(
            functools.partial(body, R, Z, bpd, states, height, breadth, ne),
            out_shape=jax.ShapeDtypeStruct((ne, spc), jnp.float32),
            in_specs=[smem, smem, any_space, any_space, any_space],
            out_specs=pl.BlockSpec(memory_space=pltpu.VMEM),
            scratch_shapes=[
                pltpu.VMEM((ne, height, breadth), jnp.bfloat16),
                pltpu.VMEM((R, bpd * states, breadth), jnp.bfloat16),
                pltpu.VMEM((R, bpd * states, height), jnp.bfloat16),
                pltpu.VMEM((2, rows, breadth), jnp.float32),
                pltpu.VMEM((2, rows, breadth), jnp.float32),
                pltpu.VMEM((ne, states, LANES), jnp.float32),
                pltpu.VMEM((Z, ne, spc, LANES), jnp.float32),
                pltpu.VMEM((max(Z - 1, 1), ne, spc, LANES), jnp.float32),
                pltpu.VMEM((R, ne, spc, LANES), jnp.float32),
                pltpu.VMEM((Z, bpd // 2 * states, breadth), jnp.bfloat16),
                dma((2, 2)), dma, dma((units,)), dma((units,)), dma((units,)),
                dma((units,)), dma((units,)),
                dma((Z,)), dma((Z,)), dma((R,)), dma((R,)),
                dma((Z * bpd,)), dma((Z * bpd,)), dma((Z * bpd * R // Z,)),
            ],
            compiler_params=pltpu.CompilerParams(
                collective_id=0, has_side_effects=True, vmem_limit_bytes=62 * 1024 * 1024),
            name="pole_sigma",
        )(frequency_grid, band_energy, eps_static, eps_imag,
          pair_elements.reshape(bpd * states, breadth))

    return jax.shard_map(
        shards,
        mesh=mesh,
        in_specs=(P("grow", "gcol"), P("grow", "gcol"), P(), P(), P("grow", None, "gcol")),
        out_specs=P(None, "gcol"),
        check_vma=False,
    )
```

profile of v0, /device:TPU:0, one launch (start us, length us, event | category | flops | bytes accessed | tf_op | source)
XLA Modules:
  0.0 171.4 jit_solution(8538399631790866492)
XLA Ops:
  0.0 170.1 %pole_sigma.1 = f32[3,16]{1,0:T(4,128)} custom-call(f32[3]{0:T(128)} %freq.1, f32[32]{0:T(128)} %energy.1, f32[1536,3072]{1,0:T(8,128)} %es_hbm.1, f32[1536,3072]{1,0:T(8,128)} %ei_hbm.1, bf16[256,3072]{1,0:T(8,128)(2,1)} %bitcast.1), custom_call_target="tpu_custom_call" | custom-call | tf_op jit(solution)/shard_map/pole_sigma/pallas_call | solution.py:363
  170.1 1.3 copy.7
where the time goes:
time: 172 us; the launch traced here: 171 us
  Pallas kernels  170 us (99%)
    pallas_call x1, Pallas kernels, shards(): pl.pallas_call(functools.partial(body, R, Z, bpd, states, height, breadth...  170 us

commit v1 on v0

v1 whole, which is shorter than its diff:
```python
import functools

import jax
import jax.numpy as jnp
from jax import lax
from jax.experimental import pallas as pl
from jax.experimental.pallas import tpu as pltpu
from jax.sharding import PartitionSpec as P

LANES = 128
SUB_ROWS = 32
SUB_COLS = 512
DOT_ROWS = 128
DOT_COLS = 1536
BUILD_RATE = 2
PIECE_RATE = 2
LEAD = 4


def bit_flip(index, mask, extent):
    total, bit = 0, 1
    while bit < extent:
        total = total + ((index // bit + mask // bit) % 2) * bit
        bit *= 2
    return total


def flag(condition):
    return jnp.where(condition, 1, 0)


def count(table, tick):
    total = 0
    for entry in table:
        total = total + flag(tick >= entry)
    return total


def look(table, index):
    value = table[0]
    for n in range(1, len(table)):
        value = jnp.where(index >= n, table[n], value)
    return value


def rising(ticks):
    out = []
    for tick in ticks:
        out.append(max(tick, out[-1] if out else tick))
    return out


class Plan:
    def __init__(self, R, Z, bpd, states, breadth, blocks):
        ratio = R // Z
        self.mains, self.asides = (R - ratio) * bpd, ratio * bpd
        levels = {}
        for shard in range(R):
            levels.setdefault(bin(shard // 2).count("1"), []).append(shard)
        self.col_order, self.col_ticks = [], []
        tick = 0
        for level in sorted(levels):
            shards = sorted(levels[level], key=lambda shard: (shard % 2, shard))
            if level == 0:
                found = [b + bpd * shard for shard in shards for b in range(bpd)]
                ticks = [n // 4 for n in range(len(found))]
                tick = 2 * bpd // 2
            else:
                found = [b + bpd * shard for b in range(bpd) for shard in shards]
                each = 2 if level == 1 else 1
                ticks = [tick + n // each for n in range(len(found))]
                tick = ticks[-1] + 1
            self.col_order += found
            self.col_ticks += ticks
        due = dict(zip(self.col_order, self.col_ticks))
        main_due = [due[j] if j < ratio * bpd else max(due[j], due[j + ratio * bpd]) for j in range(self.mains)]
        self.home_ticks = rising([max(0, j - LEAD, main_due[j]) for j in range(self.mains)])
        aside_due = [max(due[k + bpd * ratio * c] for c in range(1, Z)) for k in range(self.asides)]
        step = Z - 1
        early = 2
        self.relay_pass, self.relay_end = [], []
        for d in range(Z):
            self.relay_pass.append([2 * d + (i if i <= early else early + step * (i - early) - 1) for i in range(self.asides)])
            spread = [step * i + d + 1 for i in range(self.asides)]
            self.relay_end.append(rising([max(tick, 4 * d - 3 + 2 * i) if d else tick for i, tick in enumerate(spread)]))
        self.aside_ticks = rising([max(t[k] for t in self.relay_end[1:]) + 3 for k in range(self.asides)])
        self.gb = max(1, min(bpd, DOT_ROWS // states))
        self.gps = bpd // self.gb
        found = []
        for g in range(self.mains // self.gb):
            units = range(g * self.gb, (g + 1) * self.gb)
            found.append((units[-1], max(main_due[j] for j in units), 2 * g))
        for g in range(self.asides // self.gb):
            units = range(g * self.gb, (g + 1) * self.gb)
            found.append((0, max([self.aside_ticks[units[-1]]] + [aside_due[k] for k in units]), 2 * g + 1))
        found.sort(key=lambda entry: (max(entry[0] + 2, entry[1]), entry[0]))
        self.groups = [entry[2] for entry in found]
        self.row_need = rising([entry[0] for entry in found])
        self.col_need = rising([entry[1] for entry in found])
        self.ticks = max(self.mains + Z + 1, self.row_need[-1] + Z + 2, self.col_need[-1] + 2,
                         max(t[-1] for t in self.relay_pass) + 1, max(t[-1] for t in self.relay_end) + 1)
        self.build_ticks = -(-blocks // BUILD_RATE)


def body(R, Z, bpd, states, height, breadth, ne,
         freq, energy, es_hbm, ei_hbm, pair_hbm, out,
         kern, colp, rowp, es_buf, ei_buf, sig, part, recv1, recv2, hold,
         eps_sem, own_sem, col_send, col_recv, row_recv, up_send, dn_send,
         s1_send, s1_recv, s2_send, s2_recv, hold_send, hold_recv, give_send):
    r = lax.axis_index("grow")
    z = lax.axis_index("gcol")
    ratio = R // Z
    home = r // ratio
    core = r % ratio
    offset = pl.multiple_of(core * height, height)
    spc = states // Z
    units = R * bpd
    blocks = 4 * bpd
    rows = height // blocks
    plan = Plan(R, Z, bpd, states, breadth, blocks)

    def dev(row, col):
        return dict(device_id={"grow": row, "gcol": col}, device_id_type=pl.DeviceIdType.MESH)

    def eps_copies(block, slot):
        at = pl.multiple_of(block * rows, rows)
        return (pltpu.make_async_copy(es_hbm.at[pl.ds(at, rows), :], es_buf.at[slot], eps_sem.at[0, slot]),
                pltpu.make_async_copy(ei_hbm.at[pl.ds(at, rows), :], ei_buf.at[slot], eps_sem.at[1, slot]))

    own = pltpu.make_async_copy(pair_hbm, colp.at[0], own_sem)
    own.start()
    for copy in eps_copies(0, 0):
        copy.start()

    barrier = pltpu.get_barrier_semaphore()
    for d in range(1, R):
        pl.semaphore_signal(barrier, inc=1, **dev((r + d) % R, z))
    for d in range(1, Z):
        pl.semaphore_signal(barrier, inc=1, **dev(r, (z + d) % Z))
    sig[...] = jnp.zeros_like(sig)
    own.wait()
    pl.semaphore_wait(barrier, R + Z - 2)

    def unit_rows(b):
        return pl.ds(pl.multiple_of(b * states, states), states)

    def col_copy(src_shard, dst_shard, b, row, sems=0):
        return pltpu.make_async_remote_copy(
            src_ref=colp.at[src_shard, unit_rows(b), :], dst_ref=colp.at[dst_shard, unit_rows(b), :],
            send_sem=col_send.at[sems * units + dst_shard * bpd + b], recv_sem=col_recv.at[dst_shard * bpd + b],
            **dev(row, z))

    partner = bit_flip(r, 1, R)
    bits = []
    while 2 ** (len(bits) + 1) < R:
        bits.append(2 ** (len(bits) + 1))

    top = bits[-1] if bits else 1
    heavy = jnp.where(2 * z < Z, 0, Z - 1)
    is_heavy = home == heavy

    def backward(shard):
        return (r // top + shard // top) % 2 == (heavy * ratio // top) % 2

    def send_own(b, carry):
        for bit in [1] + bits[1:]:
            col_copy(0, bit, b, bit_flip(r, bit, R)).start()
        return carry
    lax.fori_loop(0, bpd, send_own, 0)

    def send_near(b, carry):
        col_copy(0, bits[0], b, bit_flip(r, bits[0], R)).start()
        return carry

    at_home = z == home
    goes_up = jnp.logical_and(z >= home, z < Z - 1)
    goes_down = jnp.logical_and(z <= home, z > 0)
    upper = (z + 1) % Z
    lower = (z + Z - 1) % Z
    hops = jnp.where(z > home, z - home, home - z)
    lag = jnp.where(at_home, 0, hops + 1)
    skip_up = bit_flip(home, Z - 1, Z) * ratio
    skip_down = home * ratio
    skip = jnp.where(at_home, R - ratio, jnp.where(z < home, skip_down, skip_up))

    def main_shard(m, skipped):
        return m + ratio * flag(m >= skipped)

    def aside_shard(a):
        return skip + a

    def row_copy(shard, b, sems, col):
        u = shard * bpd + b
        ref = rowp.at[shard, unit_rows(b), :]
        return pltpu.make_async_remote_copy(
            src_ref=ref, dst_ref=ref, send_sem=sems.at[u], recv_sem=row_recv.at[u], **dev(r, col))

    def home_copy(shard, b, sems, col):
        u = shard * bpd + b
        return pltpu.make_async_remote_copy(
            src_ref=colp.at[shard, unit_rows(b), pl.ds(offset, height)], dst_ref=rowp.at[shard, unit_rows(b), :],
            send_sem=sems.at[u], recv_sem=row_recv.at[u], **dev(r, col))

    def col_event(n, carry):
        u = look(plan.col_order, n)
        shard, b = u // bpd, u % bpd

        @pl.when(shard >= 1)
        def _():
            col_copy(0, shard, b, partner).wait_recv()

        @pl.when(jnp.logical_and(shard >= 2, shard % 2 == 0))
        def _():
            col_copy(shard, shard + 1, b, partner).start()
            for bit in bits[1:]:
                @pl.when(jnp.logical_and(shard < bit, jnp.logical_not(backward(shard))))
                def _(bit=bit):
                    col_copy(shard, shard + bit, b, bit_flip(r, bit, R)).start()
            for bit in bits[:-1]:
                @pl.when(jnp.logical_and(shard % (2 * bit) == 0, backward(shard)))
                def _(bit=bit):
                    col_copy(shard, shard + bit, b, bit_flip(r, bit, R), 1).start()

        @pl.when(at_home)
        def _():
            local = pltpu.make_async_copy(
                colp.at[shard, unit_rows(b), pl.ds(offset, height)],
                rowp.at[shard, unit_rows(b), :], row_recv.at[u])
            local.start()
            local.wait()
        return carry

    def home_event(j, carry):
        m, b = j // bpd, j % bpd

        @pl.when(goes_up)
        def _():
            home_copy(main_shard(m, skip_up), b, up_send, upper).start()

        @pl.when(goes_down)
        def _():
            home_copy(main_shard(m, skip_down), b, dn_send, lower).start()
        return carry

    def main_event(j, carry):
        shard, b = main_shard(j // bpd, skip), j % bpd
        row_copy(shard, b, up_send, upper).wait_recv()

        @pl.when(goes_up)
        def _():
            row_copy(shard, b, up_send, upper).start()

        @pl.when(goes_down)
        def _():
            row_copy(shard, b, dn_send, lower).start()
        return carry

    def aside_event(k, carry):
        row_copy(aside_shard(k // bpd), k % bpd, up_send, upper).wait_recv()
        return carry

    relay_down = home == 0
    relays = jnp.logical_or(relay_down, home == Z - 1)
    ahead = jnp.where(relay_down, z - 1, z + 1)
    has_ahead = jnp.logical_and(relays, jnp.logical_and(ahead >= 0, ahead < Z))
    ahead_col = (ahead + Z) % Z
    ends = jnp.logical_and(relays, jnp.logical_not(has_ahead))

    def hold_rows(i):
        return pl.ds(pl.multiple_of(i * states, states), states)

    def hold_copy(d, i):
        if d == 0:
            src = colp.at[i // bpd, unit_rows(i % bpd), pl.ds(offset, height)]
        else:
            src = hold.at[d - 1, hold_rows(i), :]
        return pltpu.make_async_remote_copy(
            src_ref=src, dst_ref=hold.at[min(d, Z - 2), hold_rows(i), :],
            send_sem=hold_send.at[d * plan.asides + i], recv_sem=hold_recv.at[min(d, Z - 2) * plan.asides + i],
            **dev(r, ahead_col))

    def give_copy(d, i, panel):
        to = panel * ratio + core
        shard = bit_flip(panel, home, Z) * ratio + i // bpd
        return pltpu.make_async_remote_copy(
            src_ref=hold.at[d - 1, hold_rows(i), :], dst_ref=rowp.at[shard, unit_rows(i % bpd), :],
            send_sem=give_send.at[(d - 1) * plan.asides + i], recv_sem=row_recv.at[shard * bpd + i % bpd],
            **dev(to, z))

    def panel_of(d):
        return jnp.where(relay_down, z + d, z - d)

    def holds(d):
        return jnp.logical_and(relays, jnp.logical_and(panel_of(d) >= 0, panel_of(d) < Z))

    def relay(tick):
        for d in range(Z):
            def item(i, carry, d=d):
                if d == 0:
                    hold_copy(d, i).start()
                    return carry
                hold_copy(d - 1, i).wait_recv()

                @pl.when(has_ahead)
                def _():
                    hold_copy(d, i).start()
                give_copy(d, i, (panel_of(d) + Z) % Z).start()
                return carry

            passing = (count(plan.relay_pass[d], tick - 1), count(plan.relay_pass[d], tick))
            if d == 0:
                live = has_ahead
                lo, hi = passing
            else:
                live = holds(d)
                lo = jnp.where(ends, count(plan.relay_end[d], tick - 1), passing[0])
                hi = jnp.where(ends, count(plan.relay_end[d], tick), passing[1])

            @pl.when(jnp.logical_and(live, hi > lo))
            def _():
                lax.fori_loop(lo, hi, item, 0)

    diagonal = r * height - z * breadth
    sub_rows = min(SUB_ROWS, rows)
    sub_cols = min(SUB_COLS, breadth)
    col_steps = breadth // sub_cols
    f0, f1, f2 = freq[0], freq[1], freq[2]

    def make_block(block, carry):
        slot = block % 2

        @pl.when(block + 1 < blocks)
        def _():
            for copy in eps_copies(block + 1, 1 - slot):
                copy.start()
        for copy in eps_copies(block, slot):
            copy.wait()
        base = pl.multiple_of(block * rows, rows)

        def chunk(n, carry):
            at_row = pl.multiple_of(n // col_steps * sub_rows, sub_rows)
            at_col = pl.multiple_of(n % col_steps * sub_cols, sub_cols)
            where = (pl.ds(at_row, sub_rows), pl.ds(at_col, sub_cols))
            gap = (lax.broadcasted_iota(jnp.int32, (sub_rows, sub_cols), 0)
                   - lax.broadcasted_iota(jnp.int32, (sub_rows, sub_cols), 1))
            one = jnp.where(gap == at_col - at_row - base - diagonal, 1.0, 0.0)
            static = es_buf[(slot,) + where] - one
            imag = ei_buf[(slot,) + where] - one
            spread = static - imag
            over = imag * imag + 0.25
            under = spread * spread + 0.25
            pole = over * lax.rsqrt(over * under)
            p0, p1, p2 = pole + f0, pole + f1, pole + f2
            p01 = p0 * p1
            scale = -static * pole / (p01 * p2)
            to = (pl.ds(pl.multiple_of(base + at_row, sub_rows), sub_rows), where[1])
            kern[(0,) + to] = (p1 * p2 * scale).astype(jnp.bfloat16)
            kern[(1,) + to] = (p0 * p2 * scale).astype(jnp.bfloat16)
            kern[(2,) + to] = (p01 * scale).astype(jnp.bfloat16)
            return carry
        lax.fori_loop(0, rows // sub_rows * col_steps, chunk, 0)
        return carry

    gb, gps = plan.gb, plan.gps
    group_rows = gb * states
    dot_cols = min(DOT_COLS, breadth)
    while breadth % dot_cols:
        dot_cols //= 2
    cuts = breadth // dot_cols

    def piece(number, carry):
        code, q = look(plan.groups, number // cuts), number % cuts
        index, is_aside = code // 2, code % 2
        shard = jnp.where(is_aside == 1, aside_shard(index // gps), main_shard(index // gps, skip))
        part_of = index % gps
        first = bit_flip(r, shard, R) * bpd + part_of * gb
        at = pl.ds(pl.multiple_of(part_of * group_rows, group_rows), group_rows)
        cols = pl.ds(pl.multiple_of(q * dot_cols, dot_cols), dot_cols)
        right = colp[shard, at, cols].astype(jnp.float32)
        left = rowp[shard, at, :]
        for e in range(ne):
            prod = jnp.dot(left, kern[e, :, cols], preferred_element_type=jnp.float32) * right
            thin = prod[:, :LANES]
            for k in range(1, dot_cols // LANES):
                thin = thin + prod[:, k * LANES:(k + 1) * LANES]
            total = sig[e]
            for b in range(gb):
                miss = jnp.full((8, LANES), freq[e] - energy[first + b], jnp.float32)
                weight = (1.0 / (1.0 + miss * miss))[:1]
                total = total + weight * thin[b * states:(b + 1) * states]
            sig[e] = total
        return carry

    pieces = len(plan.groups) * cuts

    def pieces_by(tick):
        ready = jnp.minimum(count(plan.row_need, tick - lag), count(plan.col_need, tick)) * cuts
        pace = jnp.maximum(PIECE_RATE * (tick - plan.build_ticks + 1), 0)
        return jnp.minimum(ready, pace)

    def at_most(value, most):
        return jnp.minimum(jnp.maximum(value, 0), most)

    def tick_step(tick, carry):
        if bits:
            paced = at_most(tick // 2 + 1, bpd)
            lax.fori_loop(jnp.where(is_heavy, at_most((tick + 1) // 2, bpd), jnp.where(tick == 0, 0, bpd)),
                          jnp.where(is_heavy, paced, bpd), send_near, 0)
        lax.fori_loop(count(plan.col_ticks, tick - 1), count(plan.col_ticks, tick), col_event, 0)

        @pl.when(at_home)
        def _():
            lax.fori_loop(count(plan.home_ticks, tick - 1), count(plan.home_ticks, tick), home_event, 0)

        @pl.when(jnp.logical_not(at_home))
        def _():
            since = tick - lag + 1
            lax.fori_loop(at_most(since - 1, plan.mains), at_most(since, plan.mains), main_event, 0)
            lax.fori_loop(count(plan.aside_ticks, tick - 1), count(plan.aside_ticks, tick), aside_event, 0)

        relay(tick)
        lax.fori_loop(at_most(BUILD_RATE * tick, blocks), at_most(BUILD_RATE * (tick + 1), blocks), make_block, 0)
        lax.fori_loop(pieces_by(tick - 1), pieces_by(tick), piece, 0)
        return carry
    ticks = plan.ticks
    while PIECE_RATE * (ticks - plan.build_ticks) < pieces:
        ticks += 1
    lax.fori_loop(0, ticks, tick_step, 0)

    for owner in range(Z):
        for e in range(ne):
            part[owner, e] = sig[e, owner * spc:(owner + 1) * spc]

    def s1_copy(d):
        return pltpu.make_async_remote_copy(
            src_ref=part.at[(z + d) % Z], dst_ref=recv1.at[d - 1],
            send_sem=s1_send.at[d - 1], recv_sem=s1_recv.at[d - 1], **dev(r, (z + d) % Z))

    def s2_copy(d, owner):
        return pltpu.make_async_remote_copy(
            src_ref=recv2.at[owner], dst_ref=recv2.at[owner],
            send_sem=s2_send.at[d - 1], recv_sem=s2_recv.at[owner], **dev((r + d) % R, z))

    for d in range(1, Z):
        s1_copy(d).start()

    for shard in range(1, R):
        low, high = shard & -shard, 1 << (shard.bit_length() - 1)

        def drain_col(b, carry, shard=shard, sems=0):
            col_copy(0, shard, b, partner, sems).wait_send()
            return carry
        if shard % 2 or low == high:
            lax.fori_loop(0, bpd, drain_col, 0)
        else:
            @pl.when(jnp.logical_not(backward(shard - high)))
            def _(drain_col=drain_col):
                lax.fori_loop(0, bpd, drain_col, 0)

            @pl.when(backward(shard - low))
            def _(drain_col=drain_col):
                lax.fori_loop(0, bpd, functools.partial(drain_col, sems=1), 0)

    def drain_rows(j, carry):
        m, b = j // bpd, j % bpd

        @pl.when(goes_up)
        def _():
            row_copy(main_shard(m, skip_up), b, up_send, upper).wait_send()

        @pl.when(goes_down)
        def _():
            row_copy(main_shard(m, skip_down), b, dn_send, lower).wait_send()
        return carry
    lax.fori_loop(0, plan.mains, drain_rows, 0)

    for d in range(Z):
        def drain_relay(i, carry, d=d):
            @pl.when(has_ahead)
            def _():
                hold_copy(d, i).wait_send()
            if d:
                give_copy(d, i, (panel_of(d) + Z) % Z).wait_send()
            return carry

        @pl.when(has_ahead if d == 0 else holds(d))
        def _():
            lax.fori_loop(0, plan.asides, drain_relay, 0)

    mine = part[z]
    for d in range(1, Z):
        s1_copy(d).wait_recv()
        mine = mine + recv1[d - 1]
    recv2[r] = mine
    for d in range(1, R):
        s2_copy(d, r).start()
    for d in range(1, R):
        s2_copy(d, (r + R - d) % R).wait_recv()
    full = recv2[0]
    for owner in range(1, R):
        full = full + recv2[owner]
    out[...] = jnp.sum(full, axis=-1)
    for d in range(1, Z):
        s1_copy(d).wait_send()
    for d in range(1, R):
        s2_copy(d, r).wait_send()


def solution(mesh):
    R, Z = mesh.shape["grow"], mesh.shape["gcol"]

    def shards(eps_static, eps_imag, frequency_grid, band_energy, pair_elements):
        height, breadth = eps_static.shape
        bpd, states, _ = pair_elements.shape
        ne = frequency_grid.shape[0]
        spc = states // Z
        rows = height // (4 * bpd)
        dma = pltpu.SemaphoreType.DMA
        units = R * bpd
        any_space = pl.BlockSpec(memory_space=pl.ANY)
        smem = pl.BlockSpec(memory_space=pltpu.SMEM)
        return pl.pallas_call(
            functools.partial(body, R, Z, bpd, states, height, breadth, ne),
            out_shape=jax.ShapeDtypeStruct((ne, spc), jnp.float32),
            in_specs=[smem, smem, any_space, any_space, any_space],
            out_specs=pl.BlockSpec(memory_space=pltpu.VMEM),
            scratch_shapes=[
                pltpu.VMEM((ne, height, breadth), jnp.bfloat16),
                pltpu.VMEM((R, bpd * states, breadth), jnp.bfloat16),
                pltpu.VMEM((R, bpd * states, height), jnp.bfloat16),
                pltpu.VMEM((2, rows, breadth), jnp.float32),
                pltpu.VMEM((2, rows, breadth), jnp.float32),
                pltpu.VMEM((ne, states, LANES), jnp.float32),
                pltpu.VMEM((Z, ne, spc, LANES), jnp.float32),
                pltpu.VMEM((max(Z - 1, 1), ne, spc, LANES), jnp.float32),
                pltpu.VMEM((R, ne, spc, LANES), jnp.float32),
                pltpu.VMEM((max(Z - 1, 1), R // Z * bpd * states, height), jnp.bfloat16),
                dma((2, 2)), dma, dma((2 * units,)), dma((units,)), dma((units,)),
                dma((units,)), dma((units,)),
                dma((Z,)), dma((Z,)), dma((R,)), dma((R,)),
                dma((R * bpd,)), dma((R * bpd,)), dma((R * bpd,)),
            ],
            compiler_params=pltpu.CompilerParams(
                collective_id=0, has_side_effects=True, vmem_limit_bytes=63 * 1024 * 1024),
            name="pole_sigma",
        )(frequency_grid, band_energy, eps_static, eps_imag,
          pair_elements.reshape(bpd * states, breadth))

    return jax.shard_map(
        shards,
        mesh=mesh,
        in_specs=(P("grow", "gcol"), P("grow", "gcol"), P(), P(), P("grow", None, "gcol")),
        out_specs=P(None, "gcol"),
        check_vma=False,
    )
```

time: 172 us -> 160 us (0.930)
  Pallas kernels: 170 us -> 158 us
    pallas_call x1, Pallas kernels: 170 us -> 158 us  [shards(): pl.pallas_call(functools.partial(body, R, Z, bpd, states, height, breadth...]
where the time goes in v1:
time: 160 us
  Pallas kernels  158 us (99%)
    pallas_call x1, Pallas kernels, shards(): pl.pallas_call(functools.partial(body, R, Z, bpd, states, height, breadth...  158 us

profile of v1, /device:TPU:0, one launch (start us, length us, event | category | flops | bytes accessed | tf_op | source)
XLA Modules:
  0.0 159.6 jit_solution(6397248346230905056)
XLA Ops:
  0.0 158.3 %pole_sigma.1 = f32[3,16]{1,0:T(4,128)} custom-call(f32[3]{0:T(128)} %freq.1, f32[32]{0:T(128)} %energy.1, f32[1536,3072]{1,0:T(8,128)} %es_hbm.1, f32[1536,3072]{1,0:T(8,128)} %ei_hbm.1, bf16[256,3072]{1,0:T(8,128)(2,1)} %bitcast.1), custom_call_target="tpu_custom_call" | custom-call | tf_op jit(solution)/shard_map/pole_sigma/pallas_call | solution.py:522
  158.3 1.3 copy.7

commit v2 on v1

--- a/solution.py
+++ b/solution.py
@@ -12,9 +12,22 @@
 SUB_COLS = 512
 DOT_ROWS = 128
 DOT_COLS = 1536
+EARLY_COLS = 512
+EARLY_STEP = 1
+EARLY_WAIT = 1
 BUILD_RATE = 2
-PIECE_RATE = 2
-LEAD = 4
+PIECE_RATE = (3, 2)
+LEAD = 6
+COL_START = 4
+FAR_WAIT = 2
+NEAR_STEP = 1
+PASS_STEP = 2
+PASS_EARLY = 2
+END_START = 3
+END_STEP = 5
+END_BASE = -2
+ASIDE_WAIT = 1
+HOP_LAG = (3, 2)
 
 
 def bit_flip(index, mask, extent):
@@ -51,23 +64,23 @@
 
 
 class Plan:
-    def __init__(self, R, Z, bpd, states, breadth, blocks):
+    def __init__(self, R, Z, bpd, states, height, breadth, blocks):
         ratio = R // Z
         self.mains, self.asides = (R - ratio) * bpd, ratio * bpd
         levels = {}
         for shard in range(R):
             levels.setdefault(bin(shard // 2).count("1"), []).append(shard)
         self.col_order, self.col_ticks = [], []
-        tick = 0
+        tick = COL_START
         for level in sorted(levels):
             shards = sorted(levels[level], key=lambda shard: (shard % 2, shard))
             if level == 0:
                 found = [b + bpd * shard for shard in shards for b in range(bpd)]
                 ticks = [n // 4 for n in range(len(found))]
-                tick = 2 * bpd // 2
             else:
                 found = [b + bpd * shard for b in range(bpd) for shard in shards]
                 each = 2 if level == 1 else 1
+                tick += FAR_WAIT if level == 2 else 0
                 ticks = [tick + n // each for n in range(len(found))]
                 tick = ticks[-1] + 1
             self.col_order += found
@@ -77,13 +90,14 @@
         self.home_ticks = rising([max(0, j - LEAD, main_due[j]) for j in range(self.mains)])
         aside_due = [max(due[k + bpd * ratio * c] for c in range(1, Z)) for k in range(self.asides)]
         step = Z - 1
-        early = 2
         self.relay_pass, self.relay_end = [], []
         for d in range(Z):
-            self.relay_pass.append([2 * d + (i if i <= early else early + step * (i - early) - 1) for i in range(self.asides)])
-            spread = [step * i + d + 1 for i in range(self.asides)]
-            self.relay_end.append(rising([max(tick, 4 * d - 3 + 2 * i) if d else tick for i, tick in enumerate(spread)]))
-        self.aside_ticks = rising([max(t[k] for t in self.relay_end[1:]) + 3 for k in range(self.asides)])
+            self.relay_pass.append([PASS_STEP * d + i + (step - 1) * max(0, i - PASS_EARLY) for i in range(self.asides)])
+            spread = [step * i + d + END_START for i in range(self.asides)]
+            self.relay_end.append(rising([max(tick, END_STEP * d + END_BASE + 2 * i) for i, tick in enumerate(spread)]))
+        self.aside_ticks = rising([max(t[k] for t in self.relay_end[1:]) + ASIDE_WAIT for k in range(self.asides)])
+        self.near_ticks = [NEAR_STEP * b for b in range(bpd)]
+        most = self.lag(Z - 1)
         self.gb = max(1, min(bpd, DOT_ROWS // states))
         self.gps = bpd // self.gb
         found = []
@@ -93,18 +107,29 @@
         for g in range(self.asides // self.gb):
             units = range(g * self.gb, (g + 1) * self.gb)
             found.append((0, max([self.aside_ticks[units[-1]]] + [aside_due[k] for k in units]), 2 * g + 1))
-        found.sort(key=lambda entry: (max(entry[0] + 2, entry[1]), entry[0]))
+        found.sort(key=lambda entry: (max(entry[0] + self.lag(1), entry[1]), entry[0]))
+        self.last = (2 * (self.mains // self.gb - 1), 2 * (self.asides // self.gb - 1) + 1)
+        start = EARLY_WAIT + max(entry[1] for entry in found if entry[2] == self.last[0])
+        start = max(start, EARLY_WAIT + max(aside_due))
+        self.early_cols = min(EARLY_COLS, height)
+        while height % self.early_cols:
+            self.early_cols //= 2
+        self.early_ticks = [start + EARLY_STEP * n for n in range(height // self.early_cols)]
+        found = [entry for entry in found if entry[2] not in self.last]
         self.groups = [entry[2] for entry in found]
         self.row_need = rising([entry[0] for entry in found])
         self.col_need = rising([entry[1] for entry in found])
-        self.ticks = max(self.mains + Z + 1, self.row_need[-1] + Z + 2, self.col_need[-1] + 2,
-                         max(t[-1] for t in self.relay_pass) + 1, max(t[-1] for t in self.relay_end) + 1)
+        self.ticks = 1 + max(self.mains + most, self.row_need[-1] + most, self.col_need[-1] + 1, self.aside_ticks[-1], self.early_ticks[-1],
+                             max(t[-1] for t in self.relay_pass), max(t[-1] for t in self.relay_end))
         self.build_ticks = -(-blocks // BUILD_RATE)
+
+    def lag(self, hops):
+        return HOP_LAG[0] * hops // HOP_LAG[1]
 
 
 def body(R, Z, bpd, states, height, breadth, ne,
          freq, energy, es_hbm, ei_hbm, pair_hbm, out,
-         kern, colp, rowp, es_buf, ei_buf, sig, part, recv1, recv2, hold,
+         kern, colp, rowp, es_buf, ei_buf, sig, part, recv1, recv2, hold, early, stage,
          eps_sem, own_sem, col_send, col_recv, row_recv, up_send, dn_send,
          s1_send, s1_recv, s2_send, s2_recv, hold_send, hold_recv, give_send):
     r = lax.axis_index("grow")
@@ -117,7 +142,7 @@
     units = R * bpd
     blocks = 4 * bpd
     rows = height // blocks
-    plan = Plan(R, Z, bpd, states, breadth, blocks)
+    plan = Plan(R, Z, bpd, states, height, breadth, blocks)
 
     def dev(row, col):
         return dict(device_id={"grow": row, "gcol": col}, device_id_type=pl.DeviceIdType.MESH)
@@ -160,7 +185,9 @@
     is_heavy = home == heavy
 
     def backward(shard):
-        return (r // top + shard // top) % 2 == (heavy * ratio // top) % 2
+        source = bit_flip(r, shard, R)
+        corner = jnp.logical_or(source // ratio == 0, source // ratio == Z - 1)
+        return jnp.logical_or(corner, source // top % 2 == heavy * ratio // top % 2)
 
     def send_own(b, carry):
         for bit in [1] + bits[1:]:
@@ -178,7 +205,7 @@
     upper = (z + 1) % Z
     lower = (z + Z - 1) % Z
     hops = jnp.where(z > home, z - home, home - z)
-    lag = jnp.where(at_home, 0, hops + 1)
+    lag = plan.lag(hops)
     skip_up = bit_flip(home, Z - 1, Z) * ratio
     skip_down = home * ratio
     skip = jnp.where(at_home, R - ratio, jnp.where(z < home, skip_down, skip_up))
@@ -368,34 +395,67 @@
         dot_cols //= 2
     cuts = breadth // dot_cols
 
-    def piece(number, carry):
-        code, q = look(plan.groups, number // cuts), number % cuts
+    def place(code):
         index, is_aside = code // 2, code % 2
         shard = jnp.where(is_aside == 1, aside_shard(index // gps), main_shard(index // gps, skip))
         part_of = index % gps
         first = bit_flip(r, shard, R) * bpd + part_of * gb
-        at = pl.ds(pl.multiple_of(part_of * group_rows, group_rows), group_rows)
+        return shard, pl.ds(pl.multiple_of(part_of * group_rows, group_rows), group_rows), first
+
+    def gather_sum(e, prod, first):
+        thin = prod[:, :LANES]
+        for k in range(1, prod.shape[1] // LANES):
+            thin = thin + prod[:, k * LANES:(k + 1) * LANES]
+        total = sig[e]
+        for b in range(gb):
+            miss = jnp.full((8, LANES), freq[e] - energy[first + b], jnp.float32)
+            weight = (1.0 / (1.0 + miss * miss))[:1]
+            total = total + weight * thin[b * states:(b + 1) * states]
+        sig[e] = total
+
+    def piece(number, carry):
+        q = number % cuts
+        shard, at, first = place(look(plan.groups, number // cuts))
         cols = pl.ds(pl.multiple_of(q * dot_cols, dot_cols), dot_cols)
         right = colp[shard, at, cols].astype(jnp.float32)
         left = rowp[shard, at, :]
         for e in range(ne):
-            prod = jnp.dot(left, kern[e, :, cols], preferred_element_type=jnp.float32) * right
-            thin = prod[:, :LANES]
-            for k in range(1, dot_cols // LANES):
-                thin = thin + prod[:, k * LANES:(k + 1) * LANES]
-            total = sig[e]
-            for b in range(gb):
-                miss = jnp.full((8, LANES), freq[e] - energy[first + b], jnp.float32)
-                weight = (1.0 / (1.0 + miss * miss))[:1]
-                total = total + weight * thin[b * states:(b + 1) * states]
-            sig[e] = total
-        return carry
+            gather_sum(e, jnp.dot(left, kern[e, :, cols], preferred_element_type=jnp.float32) * right, first)
+        return carry
+
+    def early_piece(n, carry):
+        @pl.when(n == 0)
+        def _():
+            for half, code in enumerate(plan.last):
+                shard, at, _ = place(code)
+
+                def stage_rows(i, carry, half=half, shard=shard, at=at):
+                    step = pl.ds(pl.multiple_of(i * 16, 16), 16)
+                    to = pl.ds(pl.multiple_of(half * group_rows + i * 16, 16), 16)
+                    from_rows = pl.ds(pl.multiple_of(at.start + i * 16, 16), 16)
+                    stage[to, :] = colp[shard, from_rows, :]
+                    return carry
+                lax.fori_loop(0, group_rows // 16, stage_rows, 0)
+        some = pl.ds(pl.multiple_of(n * plan.early_cols, plan.early_cols), plan.early_cols)
+        left = stage[...]
+        for e in range(ne):
+            early[e, :, some] = lax.dot_general(
+                left, kern[e, some, :], (((1,), (1,)), ((), ())), preferred_element_type=jnp.float32).astype(jnp.bfloat16)
+        return carry
+
+    def finish():
+        for half, code in enumerate(plan.last):
+            shard, at, first = place(code)
+            right = rowp[shard, at, :].astype(jnp.float32)
+            for e in range(ne):
+                left = early[e, half * group_rows:(half + 1) * group_rows, :].astype(jnp.float32)
+                gather_sum(e, left * right, first)
 
     pieces = len(plan.groups) * cuts
 
     def pieces_by(tick):
         ready = jnp.minimum(count(plan.row_need, tick - lag), count(plan.col_need, tick)) * cuts
-        pace = jnp.maximum(PIECE_RATE * (tick - plan.build_ticks + 1), 0)
+        pace = PIECE_RATE[0] * jnp.maximum(tick - plan.build_ticks + 1, 0) // PIECE_RATE[1]
         return jnp.minimum(ready, pace)
 
     def at_most(value, most):
@@ -403,9 +463,8 @@
 
     def tick_step(tick, carry):
         if bits:
-            paced = at_most(tick // 2 + 1, bpd)
-            lax.fori_loop(jnp.where(is_heavy, at_most((tick + 1) // 2, bpd), jnp.where(tick == 0, 0, bpd)),
-                          jnp.where(is_heavy, paced, bpd), send_near, 0)
+            lax.fori_loop(jnp.where(is_heavy, count(plan.near_ticks, tick - 1), bpd * flag(tick > 0)),
+                          jnp.where(is_heavy, count(plan.near_ticks, tick), bpd), send_near, 0)
         lax.fori_loop(count(plan.col_ticks, tick - 1), count(plan.col_ticks, tick), col_event, 0)
 
         @pl.when(at_home)
@@ -421,11 +480,13 @@
         relay(tick)
         lax.fori_loop(at_most(BUILD_RATE * tick, blocks), at_most(BUILD_RATE * (tick + 1), blocks), make_block, 0)
         lax.fori_loop(pieces_by(tick - 1), pieces_by(tick), piece, 0)
+        lax.fori_loop(count(plan.early_ticks, tick - 1), count(plan.early_ticks, tick), early_piece, 0)
         return carry
     ticks = plan.ticks
-    while PIECE_RATE * (ticks - plan.build_ticks) < pieces:
+    while PIECE_RATE[0] * (ticks - plan.build_ticks) // PIECE_RATE[1] < pieces:
         ticks += 1
     lax.fori_loop(0, ticks, tick_step, 0)
+    finish()
 
     for owner in range(Z):
         for e in range(ne):
@@ -517,6 +578,7 @@
         rows = height // (4 * bpd)
         dma = pltpu.SemaphoreType.DMA
         units = R * bpd
+        pair_rows = 2 * states * max(1, min(bpd, DOT_ROWS // states))
         any_space = pl.BlockSpec(memory_space=pl.ANY)
         smem = pl.BlockSpec(memory_space=pltpu.SMEM)
         return pl.pallas_call(
@@ -535,13 +597,15 @@
                 pltpu.VMEM((max(Z - 1, 1), ne, spc, LANES), jnp.float32),
                 pltpu.VMEM((R, ne, spc, LANES), jnp.float32),
                 pltpu.VMEM((max(Z - 1, 1), R // Z * bpd * states, height), jnp.bfloat16),
+                pltpu.VMEM((ne, pair_rows, height), jnp.bfloat16),
+                pltpu.VMEM((pair_rows, breadth), jnp.bfloat16),
                 dma((2, 2)), dma, dma((2 * units,)), dma((units,)), dma((units,)),
                 dma((units,)), dma((units,)),
                 dma((Z,)), dma((Z,)), dma((R,)), dma((R,)),
                 dma((R * bpd,)), dma((R * bpd,)), dma((R * bpd,)),
             ],
             compiler_params=pltpu.CompilerParams(
-                collective_id=0, has_side_effects=True, vmem_limit_bytes=63 * 1024 * 1024),
+                collective_id=0, has_side_effects=True, vmem_limit_bytes=63 * 1024 * 1024 + 512 * 1024),
             name="pole_sigma",
         )(frequency_grid, band_energy, eps_static, eps_imag,
           pair_elements.reshape(bpd * states, breadth))

time: 160 us -> 140 us (0.88)
  Pallas kernels: 158 us -> 138 us
    pallas_call x1, Pallas kernels: 158 us -> 138 us  [shards(): pl.pallas_call(functools.partial(body, R, Z, bpd, states, height, breadth...]
where the time goes in v2:
time: 140 us; the launch traced here: 139 us
  Pallas kernels  138 us (99%)
    pallas_call x1, Pallas kernels, shards(): pl.pallas_call(functools.partial(body, R, Z, bpd, states, height, breadth...  138 us

profile of v2, /device:TPU:0, one launch (start us, length us, event | category | flops | bytes accessed | tf_op | source)
XLA Modules:
  0.0 139.2 jit_solution(6143966567157828525)
XLA Ops:
  0.0 138.0 %pole_sigma.1 = f32[3,16]{1,0:T(4,128)} custom-call(f32[3]{0:T(128)} %freq.1, f32[32]{0:T(128)} %energy.1, f32[1536,3072]{1,0:T(8,128)} %es_hbm.1, f32[1536,3072]{1,0:T(8,128)} %ei_hbm.1, bf16[256,3072]{1,0:T(8,128)(2,1)} %bitcast.1), custom_call_target="tpu_custom_call" | custom-call | tf_op jit(solution)/shard_map/pole_sigma/pallas_call | solution.py:584
  138.0 1.3 copy.7

commit v3 on v2

--- a/solution.py
+++ b/solution.py
@@ -9,7 +9,7 @@
 
 LANES = 128
 SUB_ROWS = 32
-SUB_COLS = 512
+SUB_COLS = 1536
 DOT_ROWS = 128
 DOT_COLS = 1536
 EARLY_COLS = 512
@@ -488,9 +488,9 @@
     lax.fori_loop(0, ticks, tick_step, 0)
     finish()
 
+    part[...] = jnp.zeros_like(part)
     for owner in range(Z):
-        for e in range(ne):
-            part[owner, e] = sig[e, owner * spc:(owner + 1) * spc]
+        part[owner, :ne, :spc] = jnp.sum(sig[:, owner * spc:(owner + 1) * spc, :], axis=-1)
 
     def s1_copy(d):
         return pltpu.make_async_remote_copy(
@@ -560,7 +560,7 @@
     full = recv2[0]
     for owner in range(1, R):
         full = full + recv2[owner]
-    out[...] = jnp.sum(full, axis=-1)
+    out[...] = full[:ne, :spc]
     for d in range(1, Z):
         s1_copy(d).wait_send()
     for d in range(1, R):
@@ -575,6 +575,7 @@
         bpd, states, _ = pair_elements.shape
         ne = frequency_grid.shape[0]
         spc = states // Z
+        flat, wide = -(-ne // 8) * 8, -(-spc // LANES) * LANES
         rows = height // (4 * bpd)
         dma = pltpu.SemaphoreType.DMA
         units = R * bpd
@@ -593,9 +594,9 @@
                 pltpu.VMEM((2, rows, breadth), jnp.float32),
                 pltpu.VMEM((2, rows, breadth), jnp.float32),
                 pltpu.VMEM((ne, states, LANES), jnp.float32),
-                pltpu.VMEM((Z, ne, spc, LANES), jnp.float32),
-                pltpu.VMEM((max(Z - 1, 1), ne, spc, LANES), jnp.float32),
-                pltpu.VMEM((R, ne, spc, LANES), jnp.float32),
+                pltpu.VMEM((Z, flat, wide), jnp.float32),
+                pltpu.VMEM((max(Z - 1, 1), flat, wide), jnp.float32),
+                pltpu.VMEM((R, flat, wide), jnp.float32),
                 pltpu.VMEM((max(Z - 1, 1), R // Z * bpd * states, height), jnp.bfloat16),
                 pltpu.VMEM((ne, pair_rows, height), jnp.bfloat16),
                 pltpu.VMEM((pair_rows, breadth), jnp.bfloat16),

time: 140 us -> 139 us (level)
  no operation moved by 1% of the time
where the time goes in v3:
time: 139 us; the launch traced here: 138 us
  Pallas kernels  137 us (99%)
    pallas_call x1, Pallas kernels, shards(): pl.pallas_call(functools.partial(body, R, Z, bpd, states, height, breadth...  137 us

profile of v3, /device:TPU:0, one launch (start us, length us, event | category | flops | bytes accessed | tf_op | source)
XLA Modules:
  0.0 138.3 jit_solution(17949287646568903982)
XLA Ops:
  0.0 137.1 %pole_sigma.1 = f32[3,16]{1,0:T(4,128)} custom-call(f32[3]{0:T(128)} %freq.1, f32[32]{0:T(128)} %energy.1, f32[1536,3072]{1,0:T(8,128)} %es_hbm.1, f32[1536,3072]{1,0:T(8,128)} %ei_hbm.1, bf16[256,3072]{1,0:T(8,128)(2,1)} %bitcast.1), custom_call_target="tpu_custom_call" | custom-call | tf_op jit(solution)/shard_map/pole_sigma/pallas_call | solution.py:585
  137.1 1.3 copy.7
